TPU v7x, 32 devices: a whole 2x2x4 slice. The times are simulated.
32 devices in a mesh: samp: 16 (over z, y, x), feat: 2 (over core).
Axes of the slice: x: 2, y: 2, z: 4, core: 2. Of those that a mesh axis runs over, the one named last changes fastest.
Arguments:
- design_matrix: bfloat16 [2048, 32768], P('samp', 'feat'), may hold values from -0.046875 to 0.046875
- labels: int32 [2048], P('samp'), may hold values from 0 to 1
- weights: float32 [16, 32768], P(None, ('feat', 'samp')), may hold values from -6 to 6
- lambdas: float32 [16], replicated, may hold values from 0.05 to 1
- sketch: bfloat16 [32768, 384], P(('feat', 'samp')), may hold values from -0.03125 to 0.03125
- sketch_values: float32 [384], replicated, may hold values from 0.05 to 2
Outputs:
- new_weights: float32 [16, 32768], P(None, ('feat', 'samp'))
All inputs are finite; a program needn't handle non-finite values.
Results may differ from a plain program's by a relative error of at most 0.004.
Values may be sent and summed in bfloat16 or wider, within the bound.
No kernel may reach another device: no remote copies, remote signals or barrier semaphores. Data moves between devices by JAX's collectives and lax.ppermute only.
A program may use at most 64 MiB of HBM per device.

v0:
```python
import jax
import jax.numpy as jnp
from jax import lax
from jax.sharding import PartitionSpec as P

ITERS = 2


def shards(design_matrix, labels, weights, lambdas, sketch, sketch_values):
    sketch_full = sketch.astype(jnp.float32)
    smallest = jnp.min(sketch_values)
    ratios = (smallest + lambdas[:, None]) / (sketch_values[None, :] + lambdas[:, None]) - 1.0

    def apply_rows(vector):
        vector_half = vector.astype(jnp.bfloat16)
        partial_rows = lax.dot_general(
            lax.all_gather(vector_half, "samp", axis=1, tiled=True),
            design_matrix,
            (((1,), (1,)), ((), ())),
            preferred_element_type=jnp.float32,
        )
        return lax.psum(partial_rows, "feat")

    def apply_columns(values):
        return lax.psum_scatter(
            lax.dot_general(
                design_matrix, values, (((0,), (1,)), ((), ())), preferred_element_type=jnp.float32
            ),
            "samp",
            scatter_dimension=0,
            tiled=True,
        ).T

    def precondition(residual):
        projected = jnp.dot(residual, sketch_full, precision=lax.Precision.HIGHEST)
        projected = lax.psum(projected, ("samp", "feat"))
        correction = lax.dot_general(
            ratios * projected,
            sketch_full,
            (((1,), (1,)), ((), ())),
            precision=lax.Precision.HIGHEST,
        )
        precond_res = residual + correction
        res_dot = lax.psum(jnp.sum(residual * precond_res, axis=1), ("samp", "feat"))
        return (precond_res, res_dot)

    logits = apply_rows(weights)
    probability = jax.nn.sigmoid(logits)
    hessian_diag = probability * (1.0 - probability)
    miss_rows = (probability - labels[None, :].astype(jnp.float32)).astype(jnp.bfloat16)
    gradient = apply_columns(miss_rows) + lambdas[:, None] * weights
    residual = -gradient
    precond_res, res_dot = precondition(residual)
    direction = precond_res
    update = jnp.zeros_like(residual)
    for iteration in range(ITERS):
        image_rows = apply_rows(direction)
        hess_dir = (
            apply_columns((hessian_diag * image_rows).astype(jnp.bfloat16))
            + lambdas[:, None] * direction
        )
        curvature = lax.psum(jnp.sum(direction * hess_dir, axis=1), ("samp", "feat"))
        step_size = res_dot / curvature
        update = update + step_size[:, None] * direction
        if iteration + 1 < ITERS:
            residual = residual - step_size[:, None] * hess_dir
            precond_res, new_dot = precondition(residual)
            direction = precond_res + (new_dot / res_dot)[:, None] * direction
            res_dot = new_dot
    return weights + update


def solution(mesh):
    return jax.shard_map(
        shards,
        mesh=mesh,
        in_specs=(
            P("samp", "feat"),
            P("samp"),
            P(None, ("feat", "samp")),
            P(),
            P(("feat", "samp"), None),
            P(),
        ),
        out_specs=P(None, ("feat", "samp")),
        check_vma=False,
    )
```

profile of v0, /device:TPU:10, one launch (start us, length us, event | category | flops | bytes accessed | tf_op | source)
XLA Modules:
  0.0 596.1 jit_solution(18189731865618623638)
XLA Ops:
  6.5 0.0 copy-start
  6.5 0.0 reduce-scatter.4.cloned.1.call-start
  6.5 0.7 convert_element_type.24
  7.3 0.8 convert_element_type.23
  8.1 33.0 %all_gather.9 = bf16[16,16384]{1,0:T(8,128)(2,1)S(1)} all-gather(bf16[16,1024]{1,0:T(8,128)(2,1)S(1)} %convert_element_type.23), channel_id=1, replica_groups=mesh['samp'=16,'feat'=2] {'samp'}, dimensions={1}, use_global_device_ids=true | all-gather | bytes 557056 | tf_op jit(solution)/shard_map/all_gather | solution.py:17
  41.1 3.4 fusion.22
  44.4 0.0 copy-start.3
  44.4 0.0 copy-start.2
  44.4 0.0 copy-start.1
  44.5 2.6 psum.63
  47.1 3.8 convolution_bitcast_fusion.2
  51.0 0.0 reduce-scatter.4.cloned.1.call-update
  51.0 0.0 reduce-scatter.6.cloned.1.call-start
  51.0 0.0 copy-done.3
  51.0 0.6 reduce_min.9
  51.6 0.0 copy-done.2
  51.6 0.6 broadcast_add_fusion
  52.3 73.3 %reduce-scatter.4.cloned.1.call-done = f32[1024,16]{0,1:T(8,128)} async-done(((f32[16384,16]{0,1:T(8,128)}), f32[1024,16]{0,1:T(8,128)}) %reduce-scatter.4.cloned.1.call-update) | async-done | bytes 65552 | tf_op jit(solution)/shard_map/reduce_scatter | solution.py:25
  125.6 0.0 copy-done.1
  125.6 0.9 fusion.2
  126.6 0.0 copy-done
  126.6 0.4 fusion.23
  127.0 50.1 %psum.64 = f32[16,384]{1,0:T(8,128)S(1)} all-reduce(f32[16,384]{1,0:T(8,128)S(1)} %fusion.23), channel_id=1, replica_groups=mesh['samp'=16,'feat'=2] {'samp','feat'}, use_global_device_ids=true, to_apply=%region_3.0 | all-reduce | flops 6144 | bytes 49152 | tf_op jit(solution)/shard_map/psum | solution.py:36
  177.1 0.7 fusion.21
  177.8 32.0 %all_gather.10 = bf16[16,16384]{1,0:T(8,128)(2,1)S(1)} all-gather(bf16[16,1024]{1,0:T(8,128)(2,1)S(1)} %get-tuple-element.9), channel_id=1, replica_groups=mesh['samp'=16,'feat'=2] {'samp'}, dimensions={1}, use_global_device_ids=true | all-gather | bytes 557056 | tf_op jit(solution)/shard_map/all_gather | solution.py:17
  209.8 3.4 fusion.24
  213.1 2.5 psum.66
  215.6 3.8 convolution_bitcast_fusion.1
  219.5 0.0 reduce-scatter.6.cloned.1.call-update
  219.5 0.0 reduce-scatter.8.cloned.1.call-start
  219.5 71.6 %reduce-scatter.6.cloned.1.call-done = f32[1024,16]{0,1:T(8,128)} async-done(((f32[16384,16]{0,1:T(8,128)}), f32[1024,16]{0,1:T(8,128)}) %reduce-scatter.6.cloned.1.call-update) | async-done | bytes 65552 | tf_op jit(solution)/shard_map/reduce_scatter | solution.py:25
  291.1 1.0 multiply_reduce_fusion.1
  292.1 49.7 %all-reduce = (f32[16]{0:T(128)S(1)}, f32[16]{0:T(128)S(1)}) all-reduce(f32[16]{0:T(128)S(1)} %get-tuple-element.6, f32[16]{0:T(128)S(1)} %get-tuple-element.5), channel_id=1, replica_groups=mesh['samp'=16,'feat'=2] {'samp','feat'}, use_global_device_ids=true, to_apply=%region_5.0 | all-reduce | flops 32 | bytes 256 | tf_op jit(solution)/shard_map/psum | solution.py:44
  341.9 0.9 multiply_subtract_fusion
  342.8 0.4 fusion.25
  343.2 38.3 %psum.68 = f32[16,384]{1,0:T(8,128)S(1)} all-reduce(f32[16,384]{1,0:T(8,128)S(1)} %fusion.25), channel_id=1, replica_groups=mesh['samp'=16,'feat'=2] {'samp','feat'}, use_global_device_ids=true, to_apply=%region_10.0 | all-reduce | flops 6144 | bytes 49152 | tf_op jit(solution)/shard_map/psum | solution.py:36
  381.5 0.8 multiply_reduce_fusion
  382.3 41.9 %psum.69 = f32[16]{0:T(128)S(1)} all-reduce(f32[16]{0:T(128)S(1)} %get-tuple-element.11), channel_id=1, replica_groups=mesh['samp'=16,'feat'=2] {'samp','feat'}, use_global_device_ids=true, to_apply=%region_12.0 | all-reduce | flops 16 | bytes 128 | tf_op jit(solution)/shard_map/psum | solution.py:44
  424.2 0.1 fusion.20
  424.3 31.8 %all_gather.11 = bf16[16,16384]{1,0:T(8,128)(2,1)S(1)} all-gather(bf16[16,1024]{1,0:T(8,128)(2,1)S(1)} %fusion.20), channel_id=1, replica_groups=mesh['samp'=16,'feat'=2] {'samp'}, dimensions={1}, use_global_device_ids=true | all-gather | bytes 557056 | tf_op jit(solution)/shard_map/all_gather | solution.py:17
  456.1 3.4 fusion.26
  459.5 2.5 psum.70
  462.0 3.9 convolution_bitcast_fusion
  465.8 0.0 reduce-scatter.8.cloned.1.call-update
  465.8 72.2 %reduce-scatter.8.cloned.1.call-done = f32[1024,16]{0,1:T(8,128)} async-done(((f32[16384,16]{0,1:T(8,128)}), f32[1024,16]{0,1:T(8,128)}) %reduce-scatter.8.cloned.1.call-update) | async-done | bytes 65552 | tf_op jit(solution)/shard_map/reduce_scatter | solution.py:25
  538.1 1.0 fusion.1
  539.1 49.8 %psum.71 = f32[16]{0:T(128)S(1)} all-reduce(f32[16]{0:T(128)S(1)} %fusion.1), channel_id=1, replica_groups=mesh['samp'=16,'feat'=2] {'samp','feat'}, use_global_device_ids=true, to_apply=%region_16.0 | all-reduce | flops 16 | bytes 128 | tf_op jit(solution)/shard_map/psum | solution.py:62
  588.9 0.7 add_add_fusion
  (3 shorter events, 0.0 us)
Async XLA Ops:
  6.5 120.0 %copy-start = (bf16[1024,384]{1,0:T(8,128)(2,1)S(1)}, bf16[1024,384]{1,0:T(8,128)(2,1)}, u32[]{:S(2)}) copy-start(bf16[1024,384]{1,0:T(8,128)(2,1)} %param.10) | copy-start | bytes 2359300
  6.5 119.1 %reduce-scatter.4.cloned.1.call-start = ((), (), s32[]{:S(2)}) async-start(), calls=%async_computation.3 | async-start | bytes 1114112 | tf_op jit(solution)/shard_map/reduce_scatter | solution.py:25
  44.4 6.6 %copy-start.3 = (f32[384]{0:T(512)S(1)}, f32[384]{0:T(512)}, u32[]{:S(2)}) copy-start(f32[384]{0:T(512)} %param.11) | copy-start | bytes 4612
  44.4 7.2 %copy-start.2 = (f32[16]{0:T(128)S(1)}, f32[16]{0:T(128)}, u32[]{:S(2)}) copy-start(f32[16]{0:T(128)} %param.9) | copy-start | bytes 196
  44.4 81.2 %copy-start.1 = (f32[16,1024]{1,0:T(8,128)S(1)}, f32[16,1024]{1,0:T(8,128)}, u32[]{:S(2)}) copy-start(f32[16,1024]{1,0:T(8,128)} %param.8) | copy-start | bytes 196612
  51.0 240.1 %reduce-scatter.6.cloned.1.call-start = ((), (), s32[]{:S(2)}) async-start(), calls=%async_computation.4 | async-start | bytes 1114112 | tf_op jit(solution)/shard_map/reduce_scatter | solution.py:25
  219.5 318.6 %reduce-scatter.8.cloned.1.call-start = ((), (), s32[]{:S(2)}) async-start(), calls=%async_computation.5 | async-start | bytes 1114112 | tf_op jit(solution)/shard_map/reduce_scatter | solution.py:25
Sparse Core Ops, SparseCore 0:
  51.1 74.4 reduce-scatter.3
  219.6 71.4 reduce-scatter.5
  466.0 72.0 reduce-scatter.7
where the time goes:
time: 597 us; the launch traced here: 596 us
  blocking collectives  334 us (56%)
  waiting for transfers between devices  217 us (36%)
  matrix products  24.1 us (4%)
  between operations  13.2 us (2%)
  other arithmetic  7.54 us (1%)
    reduce_scatter x3, waiting for transfers between devices, apply_columns(): lax.psum_scatter(lax.dot_general(design_matrix, values, (((0,), (1,)), ((...  217 us
    all_gather x3, blocking collectives, apply_rows(): lax.all_gather(vector_half, 'samp', axis=1, tiled=True)  96.7 us
    psum x2, blocking collectives, precondition(): lax.psum(jnp.sum(residual * precond_res, axis=1), ('samp', 'feat'))  91.6 us
    psum x2, blocking collectives, precondition(): projected = lax.psum(projected, ('samp', 'feat'))  88.3 us
    psum x1, blocking collectives, shards(): lax.psum(jnp.sum(direction * hess_dir, axis=1), ('samp', 'feat'))  49.8 us
  transfers between devices with their start and end apart: 3, of which 3 were waited for; matrix products, arithmetic and copies ran while one was open for 0% of the time, Pallas kernels for 0%

commit v1 on v0

--- a/solution.py
+++ b/solution.py
@@ -2,6 +2,7 @@
 import jax.numpy as jnp
 from jax import lax
 from jax.sharding import PartitionSpec as P
+from jax.lax import all_to_all, axis_size
 
 ITERS = 2
 
@@ -14,7 +15,15 @@
     def apply_rows(vector):
         vector_half = vector.astype(jnp.bfloat16)
         partial_rows = lax.dot_general(
-            lax.all_gather(vector_half, "samp", axis=1, tiled=True),
+            jnp.concatenate(
+                all_to_all(
+                    jnp.stack([vector_half] * axis_size("samp"), axis=0),
+                    axis_name="samp",
+                    split_axis=0,
+                    concat_axis=0,
+                ),
+                1,
+            ),
             design_matrix,
             (((1,), (1,)), ((), ())),
             preferred_element_type=jnp.float32,

time: 597 us -> 539 us (0.903)
  blocking collectives: 334 us -> 271 us
  starting transfers between devices: 0.09 us -> 7.32 us
    all_gather x3 -> x0, blocking collectives: 96.7 us -> none  [apply_rows(): lax.all_gather(vector_half, 'samp', axis=1, tiled=True)]
    all_to_all x0 -> x2, blocking collectives: none -> 33.9 us  [apply_rows(): all_to_all(jnp.stack([vector_half] * axis_size('samp'), axis=0), axis_nam...]
    reduce_scatter x3, waiting for transfers between devices: 217 us -> 201 us  [apply_columns(): lax.psum_scatter(lax.dot_general(design_matrix, values, (((0,), (1,)), ((...]
    all_to_all x0 -> x1, waiting for transfers between devices: none -> 12.9 us  [apply_rows(): all_to_all(jnp.stack([vector_half] * axis_size('samp'), axis=0), axis_nam...]
    all_to_all x0 -> x1, starting transfers between devices: none -> 7.2 us  [apply_rows(): all_to_all(jnp.stack([vector_half] * axis_size('samp'), axis=0), axis_nam...]
  transfers between devices with their start and end apart: 3 -> 4, of which waited for: 3 -> 4; matrix products, arithmetic and copies ran while one was open for 0% -> 0% of each run, Pallas kernels for 0% -> 0%
where the time goes in v1:
time: 539 us; the launch traced here: 538 us
  blocking collectives  271 us (50%)
  waiting for transfers between devices  214 us (40%)
  matrix products  24.1 us (4%)
  between operations  13.2 us (2%)
  other arithmetic  7.54 us (1%)
  starting transfers between devices  7.32 us (1%)
    reduce_scatter x3, waiting for transfers between devices, apply_columns(): lax.psum_scatter(lax.dot_general(design_matrix, values, (((0,), (1,)), ((...  201 us
    psum x2, blocking collectives, precondition(): lax.psum(jnp.sum(residual * precond_res, axis=1), ('samp', 'feat'))  91.6 us
    psum x2, blocking collectives, precondition(): projected = lax.psum(projected, ('samp', 'feat'))  88.2 us
    psum x1, blocking collectives, shards(): lax.psum(jnp.sum(direction * hess_dir, axis=1), ('samp', 'feat'))  50 us
    all_to_all x2, blocking collectives, apply_rows(): all_to_all(jnp.stack([vector_half] * axis_size('samp'), axis=0), axis_nam...  33.9 us
    all_to_all x1, waiting for transfers between devices, apply_rows(): all_to_all(jnp.stack([vector_half] * axis_size('samp'), axis=0), axis_nam...  12.9 us
    dot_general x3, matrix products, apply_columns(): lax.dot_general(design_matrix, values, (((0,), (1,)), ((), ())), preferre...  11.5 us
  transfers between devices with their start and end apart: 4, of which 4 were waited for; matrix products, arithmetic and copies ran while one was open for 0% of the time, Pallas kernels for 0%

profile of v1, /device:TPU:10, one launch (start us, length us, event | category | flops | bytes accessed | tf_op | source)
XLA Modules:
  0.0 538.2 jit_solution(7470127569740504813)
XLA Ops:
  6.5 0.0 copy-start
  6.5 0.9 convert_element_type.23
  7.5 0.8 stack.6
  8.3 7.2 %all-to-all-start = ((bf16[16,16,1024]{2,1,0:T(8,128)(2,1)}), bf16[16,16,1024]{2,1,0:T(8,128)(2,1)S(1)}, u32[]{:S(2)}, u32[]{:S(2)}) async-start(bf16[16,16,1024]{2,1,0:T(8,128)(2,1)} %stack.6), calls=%async_computation | async-start | bytes 1048576 | tf_op jit(solution)/shard_map/all_to_all | solution.py:19
  15.5 0.0 reduce-scatter.4.cloned.1.call-start
  15.5 0.7 convert_element_type.24
  16.2 12.9 %all-to-all-done = bf16[16,16,1024]{2,1,0:T(8,128)(2,1)S(1)} async-done(((bf16[16,16,1024]{2,1,0:T(8,128)(2,1)}), bf16[16,16,1024]{2,1,0:T(8,128)(2,1)S(1)}, u32[]{:S(2)}, u32[]{:S(2)}) %all-to-all-start) | async-done | bytes 524320 | tf_op jit(solution)/shard_map/all_to_all | solution.py:19
  29.1 3.4 fusion.22
  32.5 0.0 copy-start.1
  32.5 2.6 psum.63
  35.1 3.8 convolution_bitcast_fusion.2
  39.0 0.0 reduce-scatter.4.cloned.1.call-update
  39.0 0.0 reduce-scatter.6.cloned.1.call-start
  39.1 0.0 copy-done.3
  39.1 0.6 reduce_min.9
  39.7 0.6 broadcast_add_fusion
  40.3 66.1 %reduce-scatter.4.cloned.1.call-done = f32[1024,16]{0,1:T(8,128)} async-done(((f32[16384,16]{0,1:T(8,128)}), f32[1024,16]{0,1:T(8,128)}) %reduce-scatter.4.cloned.1.call-update) | async-done | bytes 65552 | tf_op jit(solution)/shard_map/reduce_scatter | solution.py:34
  106.5 0.0 copy-done.1
  106.5 0.9 fusion.2
  107.4 0.4 fusion.23
  107.8 50.0 %psum.64 = f32[16,384]{1,0:T(8,128)S(1)} all-reduce(f32[16,384]{1,0:T(8,128)S(1)} %fusion.23), channel_id=1, replica_groups=mesh['samp'=16,'feat'=2] {'samp','feat'}, use_global_device_ids=true, to_apply=%region_3.0 | all-reduce | flops 6144 | bytes 49152 | tf_op jit(solution)/shard_map/psum | solution.py:45
  157.8 0.7 fusion.21
  158.5 0.1 stack.7
  158.6 17.0 %all_to_all.15 = bf16[16,16,1024]{2,1,0:T(8,128)(2,1)S(1)} all-to-all(bf16[16,16,1024]{2,1,0:T(8,128)(2,1)S(1)} %stack.7), channel_id=1, replica_groups=mesh['samp'=16,'feat'=2] {'samp'}, dimensions={0} | all-to-all | bytes 1048576 | tf_op jit(solution)/shard_map/all_to_all | solution.py:19
  175.6 3.4 fusion.24
  179.0 2.5 psum.66
  181.5 3.8 convolution_bitcast_fusion.1
  185.3 0.0 reduce-scatter.6.cloned.1.call-update
  185.3 0.0 reduce-scatter.8.cloned.1.call-start
  185.4 67.4 %reduce-scatter.6.cloned.1.call-done = f32[1024,16]{0,1:T(8,128)} async-done(((f32[16384,16]{0,1:T(8,128)}), f32[1024,16]{0,1:T(8,128)}) %reduce-scatter.6.cloned.1.call-update) | async-done | bytes 65552 | tf_op jit(solution)/shard_map/reduce_scatter | solution.py:34
  252.8 1.0 multiply_reduce_fusion.1
  253.8 49.7 %all-reduce = (f32[16]{0:T(128)S(1)}, f32[16]{0:T(128)S(1)}) all-reduce(f32[16]{0:T(128)S(1)} %get-tuple-element.6, f32[16]{0:T(128)S(1)} %get-tuple-element.5), channel_id=1, replica_groups=mesh['samp'=16,'feat'=2] {'samp','feat'}, use_global_device_ids=true, to_apply=%region_5.0 | all-reduce | flops 32 | bytes 256 | tf_op jit(solution)/shard_map/psum | solution.py:53
  303.5 0.9 multiply_subtract_fusion
  304.4 0.4 fusion.25
  304.9 38.3 %psum.68 = f32[16,384]{1,0:T(8,128)S(1)} all-reduce(f32[16,384]{1,0:T(8,128)S(1)} %fusion.25), channel_id=1, replica_groups=mesh['samp'=16,'feat'=2] {'samp','feat'}, use_global_device_ids=true, to_apply=%region_10.0 | all-reduce | flops 6144 | bytes 49152 | tf_op jit(solution)/shard_map/psum | solution.py:45
  343.1 0.8 multiply_reduce_fusion
  344.0 41.9 %psum.69 = f32[16]{0:T(128)S(1)} all-reduce(f32[16]{0:T(128)S(1)} %get-tuple-element.11), channel_id=1, replica_groups=mesh['samp'=16,'feat'=2] {'samp','feat'}, use_global_device_ids=true, to_apply=%region_12.0 | all-reduce | flops 16 | bytes 128 | tf_op jit(solution)/shard_map/psum | solution.py:53
  385.9 0.1 fusion.20
  386.0 0.1 stack.8
  386.0 16.9 %all_to_all.16 = bf16[16,16,1024]{2,1,0:T(8,128)(2,1)S(1)} all-to-all(bf16[16,16,1024]{2,1,0:T(8,128)(2,1)S(1)} %stack.8), channel_id=1, replica_groups=mesh['samp'=16,'feat'=2] {'samp'}, dimensions={0} | all-to-all | bytes 1048576 | tf_op jit(solution)/shard_map/all_to_all | solution.py:19
  403.0 3.4 fusion.26
  406.3 2.5 psum.70
  408.8 3.9 convolution_bitcast_fusion
  412.7 0.0 reduce-scatter.8.cloned.1.call-update
  412.7 67.3 %reduce-scatter.8.cloned.1.call-done = f32[1024,16]{0,1:T(8,128)} async-done(((f32[16384,16]{0,1:T(8,128)}), f32[1024,16]{0,1:T(8,128)}) %reduce-scatter.8.cloned.1.call-update) | async-done | bytes 65552 | tf_op jit(solution)/shard_map/reduce_scatter | solution.py:34
  480.0 1.0 fusion.1
  481.0 50.0 %psum.71 = f32[16]{0:T(128)S(1)} all-reduce(f32[16]{0:T(128)S(1)} %fusion.1), channel_id=1, replica_groups=mesh['samp'=16,'feat'=2] {'samp','feat'}, use_global_device_ids=true, to_apply=%region_16.0 | all-reduce | flops 16 | bytes 128 | tf_op jit(solution)/shard_map/psum | solution.py:71
  531.0 0.7 add_add_fusion
  (10 shorter events, 0.1 us)
Async XLA Ops:
  6.5 100.9 %copy-start = (bf16[1024,384]{1,0:T(8,128)(2,1)S(1)}, bf16[1024,384]{1,0:T(8,128)(2,1)}, u32[]{:S(2)}) copy-start(bf16[1024,384]{1,0:T(8,128)(2,1)} %param.10) | copy-start | bytes 2359300
  8.3 20.8 %all-to-all-start = ((bf16[16,16,1024]{2,1,0:T(8,128)(2,1)}), bf16[16,16,1024]{2,1,0:T(8,128)(2,1)S(1)}, u32[]{:S(2)}, u32[]{:S(2)}) async-start(bf16[16,16,1024]{2,1,0:T(8,128)(2,1)} %stack.6), calls=%async_computation | async-start | bytes 1048576 | tf_op jit(solution)/shard_map/all_to_all | solution.py:19
  15.5 91.0 %reduce-scatter.4.cloned.1.call-start = ((), (), s32[]{:S(2)}) async-start(), calls=%async_computation.6 | async-start | bytes 1114112 | tf_op jit(solution)/shard_map/reduce_scatter | solution.py:34
  32.5 6.6 %copy-start.3 = (f32[384]{0:T(512)S(1)}, f32[384]{0:T(512)}, u32[]{:S(2)}) copy-start(f32[384]{0:T(512)} %param.11) | copy-start | bytes 4612
  32.5 7.2 %copy-start.2 = (f32[16]{0:T(128)S(1)}, f32[16]{0:T(128)}, u32[]{:S(2)}) copy-start(f32[16]{0:T(128)} %param.9) | copy-start | bytes 196
  32.5 74.0 %copy-start.1 = (f32[16,1024]{1,0:T(8,128)S(1)}, f32[16,1024]{1,0:T(8,128)}, u32[]{:S(2)}) copy-start(f32[16,1024]{1,0:T(8,128)} %param.8) | copy-start | bytes 196612
  39.0 213.8 %reduce-scatter.6.cloned.1.call-start = ((), (), s32[]{:S(2)}) async-start(), calls=%async_computation.7 | async-start | bytes 1114112 | tf_op jit(solution)/shard_map/reduce_scatter | solution.py:34
  185.3 294.6 %reduce-scatter.8.cloned.1.call-start = ((), (), s32[]{:S(2)}) async-start(), calls=%async_computation.8 | async-start | bytes 1114112 | tf_op jit(solution)/shard_map/reduce_scatter | solution.py:34
Sparse Core Ops, SparseCore 0:
  39.1 67.2 reduce-scatter.3
  185.5 67.3 reduce-scatter.5
  412.8 67.1 reduce-scatter.7
